TPU v7x, 64 devices: a 2x2x8 block of a 4x4x8 slice. The times are simulated.
64 devices in a mesh: dp: 8 (over x, y, core), tp: 8 (over z).
Axes of the slice: x: 2, y: 2, z: 8, core: 2. Of those that a mesh axis runs over, the one named last changes fastest.
The devices are a block of a 4x4x8 slice.
Arguments:
- x: bfloat16 [10240, 7168], P(('dp', 'tp')), parts along dimension 0
- w_gate: bfloat16 [7168, 18432], P(None, 'tp')
- w_up: bfloat16 [7168, 18432], P(None, 'tp')
- w_down: bfloat16 [18432, 7168], P('tp')
Outputs:
- output: bfloat16 [10240, 7168], P(('dp', 'tp')), parts along dimension 0
There are 8 independent parts. A program takes and returns all parts, laid end to end along the dimension named above; an argument that names none is the same for every part.
All inputs are finite; a program needn't handle non-finite values.
Results may differ from a plain program's by a relative error of at most 0.016.
Values are sent between devices in bfloat16 or wider.
A program may use at most 768 MiB of HBM per device.

v0:
```python
import jax
import jax.numpy as jnp
from jax import lax
from jax.sharding import PartitionSpec as P


def solution(mesh):
    def step(x, w_gate, w_up, w_down):
        rows = lax.all_gather(x, "tp", axis=0, tiled=True)
        gate = jnp.dot(rows, w_gate, preferred_element_type=jnp.float32)
        up = jnp.dot(rows, w_up, preferred_element_type=jnp.float32)
        hidden = (jax.nn.silu(gate) * up).astype(jnp.bfloat16)
        term = jnp.dot(hidden, w_down, preferred_element_type=jnp.float32).astype(jnp.bfloat16)
        return lax.psum_scatter(term, "tp", scatter_dimension=0, tiled=True)

    return jax.shard_map(
        step,
        mesh=mesh,
        in_specs=(P(("dp", "tp"), None), P(None, "tp"), P(None, "tp"), P("tp", None)),
        out_specs=P(("dp", "tp"), None),
        check_vma=False,
    )
```

profile of v0, /device:TPU:21, one launch (start us, length us, event | category | flops | bytes accessed | tf_op | source)
XLA Modules:
  0.0 543.9 jit_solution(1808899977552446200)
XLA Ops:
  6.5 0.0 all-gather.2.cloned.1.call-start
  6.6 0.7 all-gather.2.cloned.1.call-update
  7.3 0.1 reduce-scatter.2.cloned.1.call-start
  7.4 190.1 %all-gather.2.cloned.1.call-done = bf16[1280,7168]{1,0:T(8,128)(2,1)} async-done(((bf16[160,7168]{1,0:T(8,128)(2,1)}), bf16[1280,7168]{1,0:T(8,128)(2,1)}) %all-gather.2.cloned.1.call-update) | async-done | bytes 18350096 | tf_op jit(solution)/shard_map/all_gather | solution.py:9
  197.4 51.6 %fusion.1 = f32[1280,2304]{1,0:T(8,128)} fusion(bf16[1280,7168]{1,0:T(8,128)(2,1)} %all-gather.2.cloned.1.call-done, bf16[7168,2304]{1,0:T(8,128)(2,1)} %param.5), kind=kOutput, calls=%fused_computation.3 | convolution fusion | flops 42278584320 | bytes 63176704 | tf_op jit(solution)/shard_map/dot_general | solution.py:10
  249.0 54.6 %fusion = bf16[1280,2304]{1,0:T(8,128)(2,1)S(1)} fusion(bf16[1280,7168]{1,0:T(8,128)(2,1)} %all-gather.2.cloned.1.call-done, bf16[7168,2304]{1,0:T(8,128)(2,1)} %param.6, f32[1280,2304]{1,0:T(8,128)} %fusion.1), kind=kOutput, calls=%fused_computation.2 | convolution fusion | flops 42296279040 | bytes 69074944 | tf_op jit(solution)/shard_map/dot_general | solution.py:11
  303.6 49.6 %convolution_convert_fusion = bf16[1280,7168]{1,0:T(8,128)(2,1)} fusion(bf16[1280,2304]{1,0:T(8,128)(2,1)S(1)} %fusion, bf16[2304,7168]{1,0:T(8,128)(2,1)} %param.7), kind=kOutput, calls=%fused_computation | convolution fusion | flops 42287759360 | bytes 57278464 | tf_op jit(solution)/shard_map/dot_general | solution.py:13
  353.2 0.1 reduce-scatter.2.cloned.1.call-update
  353.3 183.8 %reduce-scatter.2.cloned.1.call-done = bf16[160,7168]{1,0:T(8,128)(2,1)} async-done(((bf16[1280,7168]{1,0:T(8,128)(2,1)}), bf16[160,7168]{1,0:T(8,128)(2,1)}) %reduce-scatter.2.cloned.1.call-update) | async-done | bytes 2293776 | tf_op jit(solution)/shard_map/reduce_scatter | solution.py:14
Async XLA Ops:
  6.5 190.9 %all-gather.2.cloned.1.call-start = ((), (), s32[]{:S(2)}) async-start(), calls=%async_computation.1 | async-start | bytes 20643840 | tf_op jit(solution)/shard_map/all_gather | solution.py:9
  7.3 529.8 %reduce-scatter.2.cloned.1.call-start = ((), (), s32[]{:S(2)}) async-start(), calls=%async_computation.2 | async-start | bytes 20643840 | tf_op jit(solution)/shard_map/reduce_scatter | solution.py:14
Sparse Core Ops, SparseCore 0:
  8.9 188.4 all-gather.1
  353.4 183.6 reduce-scatter.1
where the time goes:
time: 544 us
  waiting for transfers between devices  375 us (69%)
  matrix products  156 us (29%)
  between operations  13.4 us (2%)
    all_gather x1, waiting for transfers between devices, step(): rows = lax.all_gather(x, 'tp', axis=0, tiled=True)  190 us
    reduce_scatter x1, waiting for transfers between devices, step(): return lax.psum_scatter(term, 'tp', scatter_dimension=0, tiled=True)  184 us
    dot_general x1, matrix products, step(): up = jnp.dot(rows, w_up, preferred_element_type=jnp.float32)  54.6 us
    dot_general x1, matrix products, step(): gate = jnp.dot(rows, w_gate, preferred_element_type=jnp.float32)  51.6 us
    dot_general x1, matrix products, step(): jnp.dot(hidden, w_down, preferred_element_type=jnp.float32)  49.6 us
  transfers between devices with their start and end apart: 2, of which 2 were waited for; matrix products, arithmetic and copies ran while one was open for 0% of the time, Pallas kernels for 0%

commit v1 on v0

--- a/solution.py
+++ b/solution.py
@@ -5,13 +5,18 @@
 
 
 def solution(mesh):
-    def step(x, w_gate, w_up, w_down):
+    def block(x, w_gate, w_up, w_down):
         rows = lax.all_gather(x, "tp", axis=0, tiled=True)
         gate = jnp.dot(rows, w_gate, preferred_element_type=jnp.float32)
         up = jnp.dot(rows, w_up, preferred_element_type=jnp.float32)
         hidden = (jax.nn.silu(gate) * up).astype(jnp.bfloat16)
         term = jnp.dot(hidden, w_down, preferred_element_type=jnp.float32).astype(jnp.bfloat16)
         return lax.psum_scatter(term, "tp", scatter_dimension=0, tiled=True)
+
+    def step(x, w_gate, w_up, w_down):
+        half = x.shape[0] // 2
+        parts = [block(part, w_gate, w_up, w_down) for part in (x[:half], x[half:])]
+        return jnp.concatenate(parts, axis=0)
 
     return jax.shard_map(
         step,

time: 544 us -> 421 us (0.77)
  waiting for transfers between devices: 375 us -> 235 us
  matrix products: 156 us -> 166 us
    all_gather x1 -> x2, waiting for transfers between devices: 190 us -> 117 us  [block(): rows = lax.all_gather(x, 'tp', axis=0, tiled=True)]
    reduce_scatter x1 -> x2, waiting for transfers between devices: 184 us -> 117 us  [block(): return lax.psum_scatter(term, 'tp', scatter_dimension=0, tiled=True)]
    dot_general x3 -> x6, matrix products: 156 us -> 166 us  [the longest x2 57.4 us: block(): gate = jnp.dot(rows, w_gate, preferred_element_type=jnp.float32)]
  transfers between devices with their start and end apart: 2 -> 4, of which waited for: 2 -> 4; matrix products, arithmetic and copies ran while one was open for 0% -> 39% of each run, Pallas kernels for 0% -> 0%
where the time goes in v1:
time: 421 us; the launch traced here: 420 us
  waiting for transfers between devices  235 us (56%)
  matrix products  166 us (39%)
  between operations  13.2 us (3%)
    reduce_scatter x2, waiting for transfers between devices, block(): return lax.psum_scatter(term, 'tp', scatter_dimension=0, tiled=True)  117 us
    all_gather x2, waiting for transfers between devices, block(): rows = lax.all_gather(x, 'tp', axis=0, tiled=True)  117 us
    dot_general x2, matrix products, block(): gate = jnp.dot(rows, w_gate, preferred_element_type=jnp.float32)  57.4 us
    dot_general x2, matrix products, block(): jnp.dot(hidden, w_down, preferred_element_type=jnp.float32)  54 us
    dot_general x2, matrix products, block(): up = jnp.dot(rows, w_up, preferred_element_type=jnp.float32)  54 us
  transfers between devices with their start and end apart: 4, of which 4 were waited for; matrix products, arithmetic and copies ran while one was open for 39% of the time, Pallas kernels for 0%

profile of v1, /device:TPU:21, one launch (start us, length us, event | category | flops | bytes accessed | tf_op | source)
XLA Modules:
  0.0 420.4 jit_solution(5395484457369777026)
XLA Ops:
  6.5 0.0 all-gather.3.cloned.1.call-start
  6.6 3.2 fusion
  9.8 0.1 all-gather.3.cloned.1.call-update
  9.8 0.1 all-gather.5.cloned.1.call-start
  9.9 0.7 all-gather.5.cloned.1.call-update
  10.6 0.1 reduce-scatter.3.cloned.1.call-start
  10.7 101.7 %all-gather.3.cloned.1.call-done = bf16[640,7168]{1,0:T(8,128)(2,1)} async-done(((bf16[80,7168]{1,0:T(8,128)(2,1)}), bf16[640,7168]{1,0:T(8,128)(2,1)}) %all-gather.3.cloned.1.call-update) | async-done | bytes 9175056 | tf_op jit(solution)/shard_map/all_gather | solution.py:9
  112.5 0.0 copy-start.1
  112.5 28.7 %fusion.1 = f32[640,2304]{1,0:T(8,128)} fusion(bf16[640,7168]{1,0:T(8,128)(2,1)} %all-gather.3.cloned.1.call-done, bf16[7168,2304]{1,0:T(8,128)(2,1)} %param.5), kind=kOutput, calls=%fused_computation.6 | convolution fusion | flops 21139292160 | bytes 48103424 | tf_op jit(solution)/shard_map/dot_general | solution.py:10
  141.2 0.0 copy-done.1
  141.2 27.0 %multiply_convert_fusion.1 = bf16[640,2304]{1,0:T(8,128)(2,1)S(1)} fusion(f32[640,2304]{1,0:T(8,128)} %fusion.1, bf16[640,7168]{1,0:T(8,128)(2,1)S(1)} %copy-done.1, bf16[7168,2304]{1,0:T(8,128)(2,1)} %param.6), kind=kOutput, calls=%fused_computation.3 | convolution fusion | flops 21148139520 | bytes 51052544 | tf_op jit(solution)/shard_map/dot_general | solution.py:11
  168.2 27.0 %convolution_convert_fusion.1 = bf16[640,7168]{1,0:T(8,128)(2,1)} fusion(bf16[640,2304]{1,0:T(8,128)(2,1)S(1)} %multiply_convert_fusion.1, bf16[2304,7168]{1,0:T(8,128)(2,1)} %param.7), kind=kOutput, calls=%fused_computation.1 | convolution fusion | flops 21143879680 | bytes 45154304 | tf_op jit(solution)/shard_map/dot_general | solution.py:13
  195.2 0.1 reduce-scatter.3.cloned.1.call-update
  195.3 0.1 reduce-scatter.5.cloned.1.call-start
  195.4 15.3 %all-gather.5.cloned.1.call-done = bf16[640,7168]{1,0:T(8,128)(2,1)} async-done(((bf16[80,7168]{1,0:T(8,128)(2,1)}), bf16[640,7168]{1,0:T(8,128)(2,1)}) %all-gather.5.cloned.1.call-update) | async-done | bytes 9175056 | tf_op jit(solution)/shard_map/all_gather | solution.py:9
  210.7 0.0 copy-start
  210.7 28.7 %fusion.2 = f32[640,2304]{1,0:T(8,128)} fusion(bf16[640,7168]{1,0:T(8,128)(2,1)} %all-gather.5.cloned.1.call-done, bf16[7168,2304]{1,0:T(8,128)(2,1)} %param.5), kind=kOutput, calls=%fused_computation.7 | convolution fusion | flops 21139292160 | bytes 48103424 | tf_op jit(solution)/shard_map/dot_general | solution.py:10
  239.4 0.0 copy-done
  239.4 27.0 %multiply_convert_fusion = bf16[640,2304]{1,0:T(8,128)(2,1)S(1)} fusion(f32[640,2304]{1,0:T(8,128)} %fusion.2, bf16[640,7168]{1,0:T(8,128)(2,1)S(1)} %copy-done, bf16[7168,2304]{1,0:T(8,128)(2,1)} %param.6), kind=kOutput, calls=%fused_computation.2 | convolution fusion | flops 21148139520 | bytes 51052544 | tf_op jit(solution)/shard_map/dot_general | solution.py:11
  266.4 27.0 %convolution_convert_fusion = bf16[640,7168]{1,0:T(8,128)(2,1)} fusion(bf16[640,2304]{1,0:T(8,128)(2,1)S(1)} %multiply_convert_fusion, bf16[2304,7168]{1,0:T(8,128)(2,1)} %param.7), kind=kOutput, calls=%fused_computation | convolution fusion | flops 21143879680 | bytes 45154304 | tf_op jit(solution)/shard_map/dot_general | solution.py:13
  293.5 0.1 reduce-scatter.5.cloned.1.call-update
  293.5 17.2 %reduce-scatter.3.cloned.1.call-done = bf16[80,7168]{1,0:T(8,128)(2,1)} async-done(((bf16[640,7168]{1,0:T(8,128)(2,1)}), bf16[80,7168]{1,0:T(8,128)(2,1)}) %reduce-scatter.3.cloned.1.call-update) | async-done | bytes 1146896 | tf_op jit(solution)/shard_map/reduce_scatter | solution.py:14
  310.8 100.0 %reduce-scatter.5.cloned.1.call-done = bf16[80,7168]{1,0:T(8,128)(2,1)} async-done(((bf16[640,7168]{1,0:T(8,128)(2,1)}), bf16[80,7168]{1,0:T(8,128)(2,1)}) %reduce-scatter.5.cloned.1.call-update) | async-done | bytes 1146896 | tf_op jit(solution)/shard_map/reduce_scatter | solution.py:14
  410.7 3.1 pad_maximum_fusion
Async XLA Ops:
  6.5 105.9 %all-gather.3.cloned.1.call-start = ((), (), s32[]{:S(2)}) async-start(), calls=%async_computation.2 | async-start | bytes 10321920 | tf_op jit(solution)/shard_map/all_gather | solution.py:9
  9.8 200.9 %all-gather.5.cloned.1.call-start = ((), (), s32[]{:S(2)}) async-start(), calls=%async_computation.4 | async-start | bytes 10321920 | tf_op jit(solution)/shard_map/all_gather | solution.py:9
  10.6 300.1 %reduce-scatter.3.cloned.1.call-start = ((), (), s32[]{:S(2)}) async-start(), calls=%async_computation.3 | async-start | bytes 10321920 | tf_op jit(solution)/shard_map/reduce_scatter | solution.py:14
  112.5 28.7 %copy-start.1 = (bf16[640,7168]{1,0:T(8,128)(2,1)S(1)}, bf16[640,7168]{1,0:T(8,128)(2,1)}, u32[]{:S(2)}) copy-start(bf16[640,7168]{1,0:T(8,128)(2,1)} %all-gather.3.cloned.1.call-done) | copy-start | bytes 27525124
  195.3 215.4 %reduce-scatter.5.cloned.1.call-start = ((), (), s32[]{:S(2)}) async-start(), calls=%async_computation.5 | async-start | bytes 10321920 | tf_op jit(solution)/shard_map/reduce_scatter | solution.py:14
  210.7 28.7 %copy-start = (bf16[640,7168]{1,0:T(8,128)(2,1)S(1)}, bf16[640,7168]{1,0:T(8,128)(2,1)}, u32[]{:S(2)}) copy-start(bf16[640,7168]{1,0:T(8,128)(2,1)} %all-gather.5.cloned.1.call-done) | copy-start | bytes 27525124
Sparse Core Ops, SparseCore 0:
  10.0 102.4 all-gather.2
  114.0 96.6 all-gather.4
  213.1 97.6 reduce-scatter.2
  313.0 97.6 reduce-scatter.4

commit v2 on v0

v2 whole, which is shorter than its diff:
```python
import functools

import jax
import jax.numpy as jnp
from jax import lax
from jax.experimental import pallas as pl
from jax.experimental.pallas import tpu as pltpu
from jax.sharding import PartitionSpec as P

MESH = pl.DeviceIdType.MESH
PIECES = 5
STRIPS = 7
LANES = 128
WIDE = 256
DELAY = 2


def kernel(
    n, x_ref, wg_ref, wu_ref, wd_ref, y_ref,
    xg, hid, terms, wbuf, slots, stage, own,
    x_sem, w_sem, ag_send, ag_recv, head_send, rs_send, rs_recv, y_sem,
):
    me = lax.axis_index("tp")
    peer = (lax.rem(me + 1, n), lax.rem(me + n - 1, n))
    rows, depth = x_ref.shape
    ff = wg_ref.shape[1]
    half = rows // 2
    group = n * half
    piece, strip = half // PIECES, depth // STRIPS
    far, near = n // 2, n - 1 - n // 2
    hops = ((far, near), (near, far))
    up_tiles, down_tiles = ff // LANES, depth // (2 * WIDE)
    per_strip = down_tiles // STRIPS

    def at(offset):
        return lax.rem(me + offset + 2 * n, n)

    def upstream(way, k):
        return at(-k) if way == 0 else at(k)

    def downstream(way, k):
        return at(k) if way == 0 else at(-k)


    def gather_copy(h, way, chunk, p, a):
        span = pl.ds(pl.multiple_of(h * group + chunk * half + p * piece, piece), piece)
        index = a if h == 0 else a + hops[0][way] * PIECES
        return pltpu.make_async_remote_copy(
            src_ref=xg.at[span],
            dst_ref=xg.at[span],
            send_sem=ag_send.at[h, way],
            recv_sem=ag_recv.at[way, index],
            device_id={"tp": peer[way]},
            device_id_type=MESH,
        )

    def gather_own(h, way):
        def send(p, _):
            gather_copy(h, way, me, p, p).start()
            return 0

        lax.fori_loop(0, PIECES, send, 0)

    def gather_event(h, way, a, forward):
        hop = lax.div(a, PIECES)
        p = a - hop * PIECES
        chunk = upstream(way, hop + 1)
        gather_copy(h, way, chunk, p, a).wait_recv()
        if forward:
            gather_copy(h, way, chunk, p, a + PIECES).start()

    def gather_sent(h, way):
        span = pl.ds(0, hops[h][way] * half)
        pltpu.make_async_remote_copy(
            src_ref=xg.at[span],
            dst_ref=xg.at[span],
            send_sem=ag_send.at[h, way],
            recv_sem=ag_recv.at[way, 0],
            device_id={"tp": peer[way]},
            device_id_type=MESH,
        ).wait_send()


    def columns(p):
        return pl.ds(pl.multiple_of(p * strip, LANES), strip)

    def of_device(d):
        return pl.ds(pl.multiple_of(d * half, 16), half)

    def box(h, way, k, p):
        first = 0 if way == 0 else hops[h][0]
        span = pl.ds(pl.multiple_of((first + k - 1) * half, 16), half)
        return (slots if h == 0 else xg).at[span, columns(p)]

    def sum_copy(h, way, k, p, src, send_sem):
        return pltpu.make_async_remote_copy(
            src_ref=src,
            dst_ref=box(h, way, k, p),
            send_sem=send_sem,
            recv_sem=rs_recv.at[h, way, (k - 1) * STRIPS + p],
            device_id={"tp": peer[way]},
            device_id_type=MESH,
        )

    def sum_wait(h, way, k, p):
        arrived = box(h, way, k, p)
        sum_copy(h, way, k, p, arrived, rs_send.at[h, way]).wait_recv()
        return arrived

    def sum_head(h, p):
        for way in range(2):
            target = downstream(way, hops[h][way])
            held = stage.at[pl.ds(way * half, half), columns(p)]
            held[...] = terms[of_device(target), columns(p)].astype(jnp.bfloat16)
            sum_copy(h, way, 1, p, held, head_send.at[h, way]).start()

    def sum_event(h, way, e):
        hop = lax.div(e, STRIPS)
        p = e - hop * STRIPS
        arrived = sum_wait(h, way, hop + 1, p)
        target = downstream(way, hops[h][way] - 1 - hop)
        term = terms[of_device(target), columns(p)]
        arrived[...] = (arrived[...].astype(jnp.float32) + term).astype(jnp.bfloat16)
        sum_copy(h, way, hop + 2, p, arrived, rs_send.at[h, way]).start()

    def sums_sent(sem, ref, count):
        span = pl.ds(0, count)
        pltpu.make_async_remote_copy(
            src_ref=ref.at[span],
            dst_ref=ref.at[span],
            send_sem=sem,
            recv_sem=rs_recv.at[0, 0, 0],
            device_id={"tp": peer[0]},
            device_id_type=MESH,
        ).wait_send()

    def finish(h, p, done):
        pltpu.make_async_copy(
            done, y_ref.at[pl.ds(h * half, half), columns(p)], y_sem.at[h]
        ).start()


    def up_copies(i, s):
        span = pl.ds(pl.multiple_of(i * LANES, LANES), LANES)
        return [
            pltpu.make_async_copy(
                ref.at[:, span], wbuf.at[s, :, pl.ds(b * LANES, LANES)], w_sem.at[s, b]
            )
            for b, ref in enumerate((wg_ref, wu_ref))
        ]

    def down_copies(j, s):
        copies = []
        for b in range(2):
            span = pl.ds(pl.multiple_of((2 * j + b) * WIDE, WIDE), WIDE)
            copies.append(
                pltpu.make_async_copy(
                    wd_ref.at[:, span], wbuf.at[s, pl.ds(b * ff, ff)], w_sem.at[s, b]
                )
            )
        return copies

    def start(copies):
        for copy in copies:
            copy.start()

    def wait(copies):
        for copy in copies:
            copy.wait()

    def gate_up(h, first, events):
        def tile(i, _):
            s = lax.rem(first + i, 2)

            @pl.when(i + 1 < up_tiles)
            def _():
                start(up_copies(i + 1, 1 - s))

            @pl.when(i + 1 == up_tiles)
            def _():
                start(down_copies(0, 1 - s))

            wait(up_copies(i, s))
            both = jnp.dot(
                xg[h * group : (h + 1) * group, :],
                wbuf[s],
                preferred_element_type=jnp.float32,
            )
            gate, up = both[:, :LANES], both[:, LANES:]
            span = pl.ds(pl.multiple_of(i * LANES, LANES), LANES)
            hid[:, span] = (jax.nn.silu(gate) * up).astype(jnp.bfloat16)
            events(i)
            return 0

        lax.fori_loop(0, up_tiles, tile, 0)

    def down(h, first, before, after):
        def one_strip(p, _):
            before(p)

            def tile(t, _):
                j = p * per_strip + t
                s = lax.rem(first + j, 2)

                @pl.when(j + 1 < down_tiles)
                def _():
                    start(down_copies(j + 1, 1 - s))

                if h == 0:

                    @pl.when(j + 1 == down_tiles)
                    def _():
                        start(up_copies(0, 1 - s))

                wait(down_copies(j, s))
                for b in range(2):
                    span = pl.ds(pl.multiple_of((2 * j + b) * WIDE, WIDE), WIDE)
                    terms[:, span] = jnp.dot(
                        hid[...],
                        wbuf[s, b * ff : (b + 1) * ff, :],
                        preferred_element_type=jnp.float32,
                    )
                return 0

            lax.fori_loop(0, per_strip, tile, 0)
            after(p)
            return 0

        lax.fori_loop(0, STRIPS, one_strip, 0)

    def spread(i, tiles, delay, count, event):
        def upto(t):
            return lax.div(jnp.maximum(t - delay, 0) * count, tiles - delay)

        def run(e, _):
            event(e)
            return 0

        lax.fori_loop(upto(i), upto(i + 1), run, 0)

    def loop(lo, hi, event):
        def run(e, _):
            event(e)
            return 0

        lax.fori_loop(lo, hi, run, 0)


    own_copies = [
        pltpu.make_async_copy(
            x_ref.at[pl.ds(h * half, half)],
            xg.at[pl.ds(pl.multiple_of(h * group + me * half, 16), half)],
            x_sem.at[h],
        )
        for h in range(2)
    ]
    start(own_copies)

    barrier = pltpu.get_barrier_semaphore()
    for other in peer:
        pl.semaphore_signal(barrier, inc=1, device_id={"tp": other}, device_id_type=MESH)
    pl.semaphore_wait(barrier, 2)

    own_copies[0].wait()
    gather_own(0, 0)
    gather_own(0, 1)
    start(up_copies(0, 0))
    own_copies[1].wait()

    def both_on(a):
        gather_event(0, 0, a, True)
        gather_event(0, 1, a, True)

    loop(0, (near - 1) * PIECES, both_on)
    gather_own(1, 1)

    def one_on(a):
        gather_event(0, 0, a, True)
        gather_event(0, 1, a, False)

    loop((near - 1) * PIECES, near * PIECES, one_on)
    gather_own(1, 0)

    def last_of_first(a):
        gather_event(0, 0, a, False)
        gather_event(1, 1, a - near * PIECES, True)

    loop(near * PIECES, far * PIECES, last_of_first)

    def second_on(j):
        gather_event(1, 0, j, True)
        gather_event(1, 1, j + PIECES, True)

    gate_up(
        0, 0,
        lambda i: spread(i, up_tiles, 0, (near - 1) * PIECES, second_on),
    )
    gather_sent(0, 0)
    gather_sent(0, 1)
    down(0, up_tiles, lambda p: None, lambda p: sum_head(0, p))

    def second_in(j):
        gather_event(1, 0, j, False)
        gather_event(1, 1, j + PIECES, False)

    loop((near - 1) * PIECES, near * PIECES, second_in)

    def first_sums(e):
        sum_event(0, 0, e)
        sum_event(0, 1, e)

    gate_up(
        1, up_tiles + down_tiles,
        lambda i: spread(i, up_tiles, min(DELAY, up_tiles - 1), (near - 1) * STRIPS, first_sums),
    )
    for way in range(2):
        sums_sent(head_send.at[0, way], stage, half)

    def near_end(p):
        sum_event(0, 0, (near - 1) * STRIPS + p)
        arrived = sum_wait(0, 1, near, p)
        own[:, columns(p)] = arrived[...].astype(jnp.float32) + terms[of_device(me), columns(p)]

    down(1, 2 * up_tiles + down_tiles, near_end, lambda p: sum_head(1, p))

    def first_end(p):
        arrived = sum_wait(0, 0, far, p)
        total = arrived[...].astype(jnp.float32) + own[:, columns(p)]
        arrived[...] = total.astype(jnp.bfloat16)
        finish(0, p, arrived)
        sum_event(1, 1, p)

    loop(0, STRIPS, first_end)

    def second_sums(e):
        sum_event(1, 1, e + STRIPS)
        sum_event(1, 0, e)

    loop(0, (near - 1) * STRIPS, second_sums)

    def second_end(p):
        one, other = sum_wait(1, 0, near, p), sum_wait(1, 1, far, p)
        total = one[...].astype(jnp.float32) + other[...].astype(jnp.float32)
        one[...] = (total + terms[of_device(me), columns(p)]).astype(jnp.bfloat16)
        finish(1, p, one)

    loop(0, STRIPS, second_end)

    for way in range(2):
        gather_sent(1, way)
        sums_sent(head_send.at[1, way], stage, half)
        for h in range(2):
            sums_sent(rs_send.at[h, way], slots, (hops[h][way] - 1) * half)
    for h in range(2):
        span = pl.ds(h * half, half)
        pltpu.make_async_copy(slots.at[pl.ds(0, half)], y_ref.at[span], y_sem.at[h]).wait()


def solution(mesh):
    n = mesh.shape["tp"]

    def step(x, w_gate, w_up, w_down):
        rows, depth = x.shape
        ff = w_gate.shape[1]
        half = rows // 2
        far = n // 2
        bf16, f32 = jnp.bfloat16, jnp.float32
        dma = pltpu.SemaphoreType.DMA
        return pl.pallas_call(
            functools.partial(kernel, n),
            name="mlp_ring",
            out_shape=jax.ShapeDtypeStruct((rows, depth), x.dtype),
            in_specs=[pl.BlockSpec(memory_space=pl.ANY)] * 4,
            out_specs=pl.BlockSpec(memory_space=pl.ANY),
            scratch_shapes=[
                pltpu.VMEM((n * rows, depth), bf16),
                pltpu.VMEM((n * half, ff), bf16),
                pltpu.VMEM((n * half, depth), f32),
                pltpu.VMEM((2, depth, WIDE), bf16),
                pltpu.VMEM(((n - 1) * half, depth), bf16),
                pltpu.VMEM((2 * half, depth), bf16),
                pltpu.VMEM((half, depth), f32),
                dma((2,)),
                dma((2, 2)),
                dma((2, 2)),
                dma((2, (n - 1) * PIECES)),
                dma((2, 2)),
                dma((2, 2)),
                dma((2, 2, far * STRIPS)),
                dma((2,)),
            ],
            compiler_params=pltpu.CompilerParams(
                collective_id=0, has_side_effects=True, vmem_limit_bytes=67043328
            ),
        )(x, w_gate, w_up, w_down)

    return jax.shard_map(
        step,
        mesh=mesh,
        in_specs=(P(("dp", "tp"), None), P(None, "tp"), P(None, "tp"), P("tp", None)),
        out_specs=P(("dp", "tp"), None),
        check_vma=False,
    )
```

time: 544 us -> 360 us (0.66)
  waiting for transfers between devices: 375 us -> 0 us
  Pallas kernels: 0 us -> 356 us
  matrix products: 156 us -> 0 us
  between operations: 13.4 us -> 0.01 us
    pallas_call x0 -> x1, Pallas kernels: none -> 356 us  [step(): pl.pallas_call(functools.partial(kernel, n), name='mlp_ring', out_shape=j...]
    all_gather x1 -> x0, waiting for transfers between devices: 190 us -> none  [step(): rows = lax.all_gather(x, 'tp', axis=0, tiled=True)]
    reduce_scatter x1 -> x0, waiting for transfers between devices: 184 us -> none  [step(): return lax.psum_scatter(term, 'tp', scatter_dimension=0, tiled=True)]
    dot_general x3 -> x0, matrix products: 156 us -> none  [the longest x1 54.6 us: step(): up = jnp.dot(rows, w_up, preferred_element_type=jnp.float32)]
  transfers between devices with their start and end apart: 2 -> 0, of which waited for: 2 -> 0; matrix products, arithmetic and copies ran while one was open for 0% -> 0% of each run, Pallas kernels for 0% -> 0%
where the time goes in v2:
time: 360 us; the launch traced here: 359 us
  Pallas kernels  356 us (99%)
    pallas_call x1, Pallas kernels, step(): pl.pallas_call(functools.partial(kernel, n), name='mlp_ring', out_shape=j...  356 us

profile of v2, /device:TPU:21, one launch (start us, length us, event | category | flops | bytes accessed | tf_op | source)
XLA Modules:
  0.0 359.3 jit_solution(11009324340132523047)
XLA Ops:
  0.0 356.2 %mlp_ring.1 = bf16[160,7168]{1,0:T(8,128)(2,1)} custom-call(bf16[160,7168]{1,0:T(8,128)(2,1)} %x_ref.1, bf16[7168,2304]{1,0:T(8,128)(2,1)} %wg_ref.1, bf16[7168,2304]{1,0:T(8,128)(2,1)} %wu_ref.1, bf16[2304,7168]{1,0:T(8,128)(2,1)} %wd_ref.1), custom_call_target="tpu_custom_call" | custom-call | tf_op jit(solution)/shard_map/mlp_ring/pallas_call | solution.py:369
  356.2 3.2 copy.6

commit v3 on v2

--- a/solution.py
+++ b/solution.py
@@ -12,13 +12,14 @@
 STRIPS = 7
 LANES = 128
 WIDE = 256
+VMEM_GRANT = 63000 * 1024
 DELAY = 2
 
 
 def kernel(
     n, x_ref, wg_ref, wu_ref, wd_ref, y_ref,
     xg, hid, terms, wbuf, slots, stage, own,
-    x_sem, w_sem, ag_send, ag_recv, head_send, rs_send, rs_recv, y_sem,
+    x_sem, w_sem, ag_send, ag_recv, head_send, rs_send, rs_recv,
 ):
     me = lax.axis_index("tp")
     peer = (lax.rem(me + 1, n), lax.rem(me + n - 1, n))
@@ -134,11 +135,6 @@
             device_id_type=MESH,
         ).wait_send()
 
-    def finish(h, p, done):
-        pltpu.make_async_copy(
-            done, y_ref.at[pl.ds(h * half, half), columns(p)], y_sem.at[h]
-        ).start()
-
 
     def up_copies(i, s):
         span = pl.ds(pl.multiple_of(i * LANES, LANES), LANES)
@@ -254,7 +250,7 @@
         )
         for h in range(2)
     ]
-    start(own_copies)
+    own_copies[0].start()
 
     barrier = pltpu.get_barrier_semaphore()
     for other in peer:
@@ -264,6 +260,7 @@
     own_copies[0].wait()
     gather_own(0, 0)
     gather_own(0, 1)
+    own_copies[1].start()
     start(up_copies(0, 0))
     own_copies[1].wait()
 
@@ -326,8 +323,7 @@
     def first_end(p):
         arrived = sum_wait(0, 0, far, p)
         total = arrived[...].astype(jnp.float32) + own[:, columns(p)]
-        arrived[...] = total.astype(jnp.bfloat16)
-        finish(0, p, arrived)
+        y_ref[pl.ds(0, half), columns(p)] = total.astype(jnp.bfloat16)
         sum_event(1, 1, p)
 
     loop(0, STRIPS, first_end)
@@ -341,8 +337,8 @@
     def second_end(p):
         one, other = sum_wait(1, 0, near, p), sum_wait(1, 1, far, p)
         total = one[...].astype(jnp.float32) + other[...].astype(jnp.float32)
-        one[...] = (total + terms[of_device(me), columns(p)]).astype(jnp.bfloat16)
-        finish(1, p, one)
+        total += terms[of_device(me), columns(p)]
+        y_ref[pl.ds(half, half), columns(p)] = total.astype(jnp.bfloat16)
 
     loop(0, STRIPS, second_end)
 
@@ -351,9 +347,6 @@
         sums_sent(head_send.at[1, way], stage, half)
         for h in range(2):
             sums_sent(rs_send.at[h, way], slots, (hops[h][way] - 1) * half)
-    for h in range(2):
-        span = pl.ds(h * half, half)
-        pltpu.make_async_copy(slots.at[pl.ds(0, half)], y_ref.at[span], y_sem.at[h]).wait()
 
 
 def solution(mesh):
@@ -369,9 +362,9 @@
         return pl.pallas_call(
             functools.partial(kernel, n),
             name="mlp_ring",
-            out_shape=jax.ShapeDtypeStruct((rows, depth), x.dtype),
+            out_shape=pltpu.VMEM((rows, depth), x.dtype),
             in_specs=[pl.BlockSpec(memory_space=pl.ANY)] * 4,
-            out_specs=pl.BlockSpec(memory_space=pl.ANY),
+            out_specs=pl.BlockSpec(memory_space=pltpu.VMEM),
             scratch_shapes=[
                 pltpu.VMEM((n * rows, depth), bf16),
                 pltpu.VMEM((n * half, ff), bf16),
@@ -387,10 +380,9 @@
                 dma((2, 2)),
                 dma((2, 2)),
                 dma((2, 2, far * STRIPS)),
-                dma((2,)),
             ],
             compiler_params=pltpu.CompilerParams(
-                collective_id=0, has_side_effects=True, vmem_limit_bytes=67043328
+                collective_id=0, has_side_effects=True, vmem_limit_bytes=VMEM_GRANT
             ),
         )(x, w_gate, w_up, w_down)
 

time: 360 us -> 357 us (level)
  no operation moved by 1% of the time
where the time goes in v3:
time: 357 us
  Pallas kernels  355 us (99%)
    pallas_call x1, Pallas kernels, step(): pl.pallas_call(functools.partial(kernel, n), name='mlp_ring', out_shape=p...  355 us

profile of v3, /device:TPU:21, one launch (start us, length us, event | category | flops | bytes accessed | tf_op | source)
XLA Modules:
  0.0 356.9 jit_solution(9791607872909493850)
XLA Ops:
  0.0 355.5 %mlp_ring.1 = bf16[160,7168]{1,0:T(8,128)(2,1)S(1)} custom-call(bf16[160,7168]{1,0:T(8,128)(2,1)} %x_ref.1, bf16[7168,2304]{1,0:T(8,128)(2,1)} %wg_ref.1, bf16[7168,2304]{1,0:T(8,128)(2,1)} %wu_ref.1, bf16[2304,7168]{1,0:T(8,128)(2,1)} %wd_ref.1), custom_call_target="tpu_custom_call" | custom-call | tf_op jit(solution)/shard_map/mlp_ring/pallas_call | solution.py:362
  355.5 1.4 copy.6

commit v4 on v3

--- a/solution.py
+++ b/solution.py
@@ -8,8 +8,8 @@
 from jax.sharding import PartitionSpec as P
 
 MESH = pl.DeviceIdType.MESH
-PIECES = 5
-STRIPS = 7
+PIECES = 2
+STRIPS = 2
 LANES = 128
 WIDE = 256
 VMEM_GRANT = 63000 * 1024
@@ -27,7 +27,7 @@
     ff = wg_ref.shape[1]
     half = rows // 2
     group = n * half
-    piece, strip = half // PIECES, depth // STRIPS
+    piece, strip = depth // PIECES, depth // STRIPS
     far, near = n // 2, n - 1 - n // 2
     hops = ((far, near), (near, far))
     up_tiles, down_tiles = ff // LANES, depth // (2 * WIDE)
@@ -44,11 +44,12 @@
 
 
     def gather_copy(h, way, chunk, p, a):
-        span = pl.ds(pl.multiple_of(h * group + chunk * half + p * piece, piece), piece)
+        span = pl.ds(pl.multiple_of(h * group + chunk * half, 16), half)
+        wide = pl.ds(pl.multiple_of(p * piece, LANES), piece)
         index = a if h == 0 else a + hops[0][way] * PIECES
         return pltpu.make_async_remote_copy(
-            src_ref=xg.at[span],
-            dst_ref=xg.at[span],
+            src_ref=xg.at[span, wide],
+            dst_ref=xg.at[span, wide],
             send_sem=ag_send.at[h, way],
             recv_sem=ag_recv.at[way, index],
             device_id={"tp": peer[way]},

time: 357 us -> 357 us (level)
  no operation moved by 1% of the time
where the time goes in v4:
time: 357 us; the launch traced here: 356 us
  Pallas kernels  355 us (99%)
    pallas_call x1, Pallas kernels, step(): pl.pallas_call(functools.partial(kernel, n), name='mlp_ring', out_shape=p...  355 us

profile of v4, /device:TPU:21, one launch (start us, length us, event | category | flops | bytes accessed | tf_op | source)
XLA Modules:
  0.0 355.9 jit_solution(875597806142168023)
XLA Ops:
  0.0 354.5 %mlp_ring.1 = bf16[160,7168]{1,0:T(8,128)(2,1)S(1)} custom-call(bf16[160,7168]{1,0:T(8,128)(2,1)} %x_ref.1, bf16[7168,2304]{1,0:T(8,128)(2,1)} %wg_ref.1, bf16[7168,2304]{1,0:T(8,128)(2,1)} %wu_ref.1, bf16[2304,7168]{1,0:T(8,128)(2,1)} %wd_ref.1), custom_call_target="tpu_custom_call" | custom-call | tf_op jit(solution)/shard_map/mlp_ring/pallas_call | solution.py:363
  354.5 1.4 copy.6
